TPU v7x, 32 devices: a whole 2x2x4 slice. The times are simulated.
32 devices in a mesh: dp: 4 (over x, y), tp: 8 (over z, core).
Axes of the slice: x: 2, y: 2, z: 4, core: 2. Of those that a mesh axis runs over, the one named last changes fastest.
Arguments:
- x_saved: bfloat16 [8, 2048, 1024], P('dp'), parts along dimension 0
- h1_saved: bfloat16 [8, 2048, 1024], P('dp'), parts along dimension 0
- grad_y: bfloat16 [8, 2048, 1024], P('dp'), parts along dimension 0
- mean_one: float32 [8, 2048], P('dp'), parts along dimension 0
- rstd_one: float32 [8, 2048], P('dp'), parts along dimension 0
- mean_two: float32 [8, 2048], P('dp'), parts along dimension 0
- rstd_two: float32 [8, 2048], P('dp'), parts along dimension 0
- gain_one: bfloat16 [1024], replicated
- gain_two: bfloat16 [1024], replicated
- w_qkv: bfloat16 [1024, 16, 3, 64], P(None, 'tp')
- w_out: bfloat16 [16, 64, 1024], P('tp')
- w_up: bfloat16 [1024, 4096], P(None, 'tp')
- w_down: bfloat16 [4096, 1024], P('tp')
Outputs:
- output 1: bfloat16 [8, 2048, 1024], P('dp'), parts along dimension 0
- output 2: bfloat16 [4096, 16, 3, 64], P('dp', 'tp'), parts along dimension 0
- output 3: bfloat16 [64, 64, 1024], P(('dp', 'tp')), parts along dimension 0
- output 4: bfloat16 [4096, 4096], P('dp', 'tp'), parts along dimension 0
- output 5: bfloat16 [16384, 1024], P(('dp', 'tp')), parts along dimension 0
There are 4 independent parts. A program takes and returns all parts, laid end to end along the dimension named above; an argument that names none is the same for every part.
All inputs are finite; a program needn't handle non-finite values.
Results may differ from a plain program's by a relative error of at most 0.0176086.
Values are sent between devices in bfloat16 or wider.
A program may use at most 1 GiB of HBM per device.

v0:
```python
import jax
import jax.numpy as jnp
from jax import lax
from jax.sharding import PartitionSpec as P
from functools import partial

GELU_C = 0.7978845608028654
GELU_A = 0.044715
wide_einsum = partial(jnp.einsum, preferred_element_type=jnp.float32)


def gelu_tanh(pre_act):
    inner_arg = GELU_C * (pre_act + GELU_A * pre_act * pre_act * pre_act)
    return 0.5 * pre_act * (1.0 + jnp.tanh(inner_arg))


def gelu_slope(pre_act):
    inner_arg = GELU_C * (pre_act + GELU_A * pre_act * pre_act * pre_act)
    tanh_val = jnp.tanh(inner_arg)
    return (0.5 * (1.0 + tanh_val)
            + 0.5 * pre_act * (1.0 - tanh_val * tanh_val) * GELU_C * (1.0 + 3.0 * GELU_A * pre_act * pre_act))


def norm_backward(grad_norm, value_a4, gain, rstd):
    scaled = grad_norm * gain.astype(jnp.float32)
    mean_scaled = jnp.mean(scaled, axis=-1, keepdims=True)
    mean_cross = jnp.mean(scaled * value_a4, axis=-1, keepdims=True)
    return rstd[..., None] * (scaled - mean_scaled - value_a4 * mean_cross)


def attention_backward(q_heads, k_heads, v_heads, grad_o, score_scale):
    seq_len = q_heads.shape[1]
    scores = wide_einsum('bqnd,bknd->bnqk', q_heads, k_heads) * score_scale
    causal = jnp.arange(seq_len)[:, None] >= jnp.arange(seq_len)[None, :]
    attn_prob = jax.nn.softmax(jnp.where(causal, scores, -1e30), axis=-1)
    prob_bf16 = attn_prob.astype(jnp.bfloat16)
    attn_out = wide_einsum('bnqk,bknd->bqnd', prob_bf16, v_heads).astype(jnp.bfloat16)
    grad_v = wide_einsum('bnqk,bqnd->bknd', prob_bf16, grad_o).astype(jnp.bfloat16)
    grad_p = wide_einsum('bqnd,bknd->bnqk', grad_o, v_heads)
    row_dot = jnp.sum(attn_prob * grad_p, axis=-1, keepdims=True)
    grad_s = (attn_prob * (grad_p - row_dot) * score_scale).astype(jnp.bfloat16)
    grad_q = wide_einsum('bnqk,bknd->bqnd', grad_s, k_heads).astype(jnp.bfloat16)
    grad_k = wide_einsum('bnqk,bqnd->bknd', grad_s, q_heads).astype(jnp.bfloat16)
    return attn_out, jnp.stack([grad_q, grad_k, grad_v], axis=3)


def solution(mesh):
    act_spec = P('dp', None, None)
    stat_spec = P('dp', None)
    in_specs = (act_spec, act_spec, act_spec, stat_spec, stat_spec, stat_spec, stat_spec, P(), P(),
                P(None, 'tp', None, None), P('tp', None, None), P(None, 'tp'), P('tp', None))
    out_specs = (act_spec, P('dp', 'tp', None, None), P(('dp', 'tp'), None, None), P('dp', 'tp'),
                 P(('dp', 'tp'), None))

    def local_backward(x_saved, h1_saved, grad_y, mean_one, rstd_one, mean_two, rstd_two,
                       gain_one, gain_two, w_qkv, w_out, w_up, w_down):
        score_scale = w_qkv.shape[3] ** -0.5
        array_b8 = (h1_saved.astype(jnp.float32) - mean_two[..., None]) * rstd_two[..., None]
        norm_two = (array_b8 * gain_two.astype(jnp.float32)).astype(jnp.bfloat16)
        pre_act = wide_einsum('msh,hf->msf', norm_two, w_up)
        act_out = gelu_tanh(pre_act).astype(jnp.bfloat16)
        grad_down = wide_einsum('msf,msh->fh', act_out, grad_y).astype(jnp.bfloat16)
        grad_pre = (wide_einsum('msh,fh->msf', grad_y, w_down) * gelu_slope(pre_act)).astype(jnp.bfloat16)
        grad_up = wide_einsum('msh,msf->hf', norm_two, grad_pre).astype(jnp.bfloat16)
        part_two = wide_einsum('msf,hf->msh', grad_pre, w_up).astype(jnp.bfloat16)
        grad_norm_two = lax.psum(part_two, 'tp').astype(jnp.float32)
        grad_h1 = (grad_y.astype(jnp.float32)
                   + norm_backward(grad_norm_two, array_b8, gain_two, rstd_two)).astype(jnp.bfloat16)
        value_a8 = (x_saved.astype(jnp.float32) - mean_one[..., None]) * rstd_one[..., None]
        norm_one = (value_a8 * gain_one.astype(jnp.float32)).astype(jnp.bfloat16)
        qkv_acts = wide_einsum('msh,hncd->msncd', norm_one, w_qkv).astype(jnp.bfloat16)
        grad_o = wide_einsum('msh,ndh->msnd', grad_h1, w_out).astype(jnp.bfloat16)
        attn_out, grad_qkv = attention_backward(qkv_acts[:, :, :, 0], qkv_acts[:, :, :, 1], qkv_acts[:, :, :, 2],
                                                grad_o, score_scale)
        grad_out_w = wide_einsum('msnd,msh->ndh', attn_out, grad_h1).astype(jnp.bfloat16)
        grad_qkv_w = wide_einsum('msh,msncd->hncd', norm_one, grad_qkv).astype(jnp.bfloat16)
        part_one = wide_einsum('msncd,hncd->msh', grad_qkv, w_qkv).astype(jnp.bfloat16)
        grad_norm_one = lax.psum(part_one, 'tp').astype(jnp.float32)
        grad_x = (grad_h1.astype(jnp.float32)
                  + norm_backward(grad_norm_one, value_a8, gain_one, rstd_one)).astype(jnp.bfloat16)
        return grad_x, grad_qkv_w, grad_out_w, grad_up, grad_down

    return jax.shard_map(local_backward, mesh=mesh, in_specs=in_specs, out_specs=out_specs, check_vma=False)
```

profile of v0, /device:TPU:0, one launch (start us, length us, event | category | flops | bytes accessed | tf_op | source)
XLA Modules:
  0.0 658.1 jit_solution(4086698081033699368)
XLA Ops:
  8.4 8.3 %fusion.37 = f32[2,2048,512]{2,1,0:T(8,128)S(1)} fusion(bf16[2,2048,1024]{2,1,0:T(8,128)(2,1)} %param.14, f32[1024]{0:T(1024)S(1)} %convert_element_type.100, f32[2,2048]{1,0:T(2,128)} %param.18, f32[2,2048]{1,0:T(2,128)} %param.19, bf16[1024,512]{1,0:T(8,128)(2,1)S(1)} %copy-done), kind=kOutput, calls=%fused_computation.50 | convolution fusion | flops 4315938816 | bytes 17862656 | tf_op jit(solution)/shard_map/msh,hf->msf/dot_general | solution.py:60
  16.7 8.9 %fusion.25 = bf16[2,2048,512]{2,1,0:T(8,128)(2,1)S(1)} fusion(f32[2,2048,512]{2,1,0:T(8,128)S(1)} %fusion.37, bf16[2,2048,1024]{2,1,0:T(8,128)(2,1)S(1)} %copy-done.7, bf16[512,1024]{1,0:T(8,128)(2,1)S(1)} %copy-done.17), kind=kOutput, calls=%fused_computation.38 | convolution fusion | flops 4334813184 | bytes 22020096 | tf_op jit(solution)/shard_map/msh,fh->msf/dot_general | solution.py:63
  27.6 6.8 %convolution_convert_fusion = bf16[2,2048,1024]{2,1,0:T(8,128)(2,1)} fusion(bf16[2,2048,512]{2,1,0:T(8,128)(2,1)S(1)} %fusion.25, bf16[1024,512]{1,0:T(8,128)(2,1)S(1)} %copy-done), kind=kOutput, calls=%fused_computation.51 | convolution fusion | flops 4299161600 | bytes 13631488 | tf_op jit(solution)/shard_map/msf,hf->msh/dot_general | solution.py:65
  34.7 4.1 iota_compare_fusion
  38.9 10.5 %bitcast_convert_fusion.2 = bf16[1024,512]{1,0:T(8,128)(2,1)} fusion(bf16[2,2048,512]{2,1,0:T(8,128)(2,1)} %copy-done.21, bf16[2,2048,1024]{2,1,0:T(8,128)(2,1)} %param.14, f32[1024]{0:T(1024)S(1)} %convert_element_type.100, f32[2,2048]{1,0:T(2,128)S(1)} %copy-done.8, f32[2,2048]{1,0:T(2,128)S(1)} %copy-done.9), kind=kOutput, calls=%fused_computation.66 | convolution fusion | flops 4316463104 | bytes 13668352 | tf_op jit(solution)/shard_map/msh,msf->hf/dot_general | solution.py:64
  49.5 6.3 fusion.39
  55.8 34.1 %fusion.102 = (f32[2,2,2048]{2,1,0:T(2,128)S(1)}, f32[2,2,2048,2048]{2,3,1,0:T(8,128)}) fusion(pred[2048,2048]{0,1:T(8,128)(4,1)} %iota_compare_fusion, bf16[2,2048,2,3,64]{1,4,3,2,0:T(8,128)(2,1)} %fusion.39), kind=kOutput, calls=%fused_computation.97 | convolution fusion | flops 2214594560 | bytes 73433088 | tf_op jit(solution)/shard_map/sub | solution.py:35
  89.9 32.7 %fusion.101 = bf16[2,2,2048,2048]{2,3,1,0:T(8,128)(2,1)} fusion(f32[2,2,2048,2048]{2,3,1,0:T(8,128)} %get-tuple-element.10, f32[2,2,2048]{2,1,0:T(2,128)S(1)} %get-tuple-element.9), kind=kLoop, calls=%fused_computation.96 | loop fusion | flops 33554432 | bytes 100696064 | tf_op jit(solution)/shard_map/convert_element_type | solution.py:36
  122.7 89.9 %all-reduce.3.cloned.1.call-done = bf16[2,2048,1024]{2,1,0:T(8,128)(2,1)} async-done(((bf16[2,2048,1024]{2,1,0:T(8,128)(2,1)}), bf16[2,2048,1024]{2,1,0:T(8,128)(2,1)}) %all-reduce.3.cloned.1.call-update) | async-done | bytes 8388624 | tf_op jit(solution)/shard_map/psum | solution.py:66
  212.6 9.3 %fusion.18 = (f32[2,2048]{1,0:T(2,128)S(1)}, f32[2,2048]{1,0:T(2,128)S(1)}) fusion(bf16[2,2048,1024]{2,1,0:T(8,128)(2,1)} %all-reduce.3.cloned.1.call-done, f32[1024]{0:T(1024)S(1)} %convert_element_type.100, f32[2,2048]{1,0:T(2,128)S(1)} %copy-done.9, f32[2,2048]{1,0:T(2,128)S(1)} %copy-done.8, bf16[2,2048,1024]{2,1,0:T(8,128)(2,1)} %param.14), kind=kLoop, calls=%fused_computation.27 | loop fusion | flops 33546240 | bytes 16846848 | tf_op jit(solution)/shard_map/reduce_sum | solution.py:26
  221.9 10.5 %add_convert_fusion.1 = bf16[2,2048,1024]{2,1,0:T(8,128)(2,1)S(1)} fusion(bf16[2,2048,1024]{2,1,0:T(8,128)(2,1)S(1)} %copy-done.5, bf16[2,2048,1024]{2,1,0:T(8,128)(2,1)} %param.14, bf16[2,2048,1024]{2,1,0:T(8,128)(2,1)} %param.15, f32[2,2048]{1,0:T(2,128)S(1)} %get-tuple-element.11, f32[2,2048]{1,0:T(2,128)S(1)} %get-tuple-element.12, ...), kind=kLoop, calls=%fused_computation.24 | loop fusion | flops 50331648 | bytes 33624064 | tf_op jit(solution)/shard_map/convert_element_type | solution.py:68
  232.5 3.2 copy-done.4
  235.7 2.9 fusion.52
  238.5 24.8 %fusion.100 = f32[2,2,2048,2048]{2,3,1,0:T(8,128)} fusion(bf16[2,2048,2,64]{1,3,2,0:T(8,128)(2,1)S(1)} %fusion.52, bf16[2,2048,2,3,64]{1,4,3,2,0:T(8,128)(2,1)} %fusion.39), kind=kOutput, calls=%fused_computation.95 | convolution fusion | flops 2147483648 | bytes 69206016 | tf_op jit(solution)/shard_map/bqnd,bknd->bnqk/dot_general | solution.py:39
  263.4 83.2 %fusion.64 = bf16[2,2048,2,1,64]{1,4,2,0,3:T(8,128)(2,1)} fusion(f32[2,2,2048,2048]{2,3,1,0:T(8,128)} %fusion.100, bf16[2,2048,2,3,64]{1,4,3,2,0:T(8,128)(2,1)} %fusion.39, f32[2,2,2048,2048]{2,3,1,0:T(8,128)} %get-tuple-element.10, f32[2,2,2048]{2,1,0:T(2,128)S(1)} %get-tuple-element.9), kind=kOutput, calls=%fused_computation.64 | convolution fusion | flops 2265458688 | bytes 270598144 | tf_op jit(solution)/shard_map/bnqk,bknd->bqnd/dot_general | solution.py:42
  346.6 83.3 %fusion.61 = bf16[2,2048,2,1,64]{1,4,2,0,3:T(8,128)(2,1)} fusion(f32[2,2,2048,2048]{2,3,1,0:T(8,128)} %fusion.100, bf16[2,2048,2,3,64]{1,4,3,2,0:T(8,128)(2,1)} %fusion.39, f32[2,2,2048,2048]{2,3,1,0:T(8,128)} %get-tuple-element.10, f32[2,2,2048]{2,1,0:T(2,128)S(1)} %get-tuple-element.9), kind=kOutput, calls=%fused_computation.63 | convolution fusion | flops 2265458688 | bytes 270598144 | tf_op jit(solution)/shard_map/bnqk,bqnd->bknd/dot_general | solution.py:43
  429.9 15.0 %fusion.55 = bf16[2,2048,2,1,64]{1,4,2,0,3:T(8,128)(2,1)S(1)} fusion(bf16[2,2048,2,64]{1,3,2,0:T(8,128)(2,1)S(1)} %copy-done.3, bf16[2,2,2048,2048]{2,3,1,0:T(8,128)(2,1)} %fusion.101), kind=kOutput, calls=%fused_computation.61 | convolution fusion | flops 2148007936 | bytes 35651584 | tf_op jit(solution)/shard_map/bnqk,bqnd->bknd/dot_general | solution.py:38
  445.0 8.6 %bitcast_convert_fusion = bf16[2,2048,1024]{2,1,0:T(8,128)(2,1)} fusion(bf16[2,2048,2,1,64]{1,4,2,0,3:T(8,128)(2,1)S(1)} %fusion.55, bf16[2,2048,2,1,64]{1,4,2,0,3:T(8,128)(2,1)} %fusion.61, bf16[2,2048,2,1,64]{1,4,2,0,3:T(8,128)(2,1)} %fusion.64, bf16[1024,2,3,64]{0,3,2,1:T(8,128)(2,1)S(1)} %copy-done.19), kind=kOutput, calls=%fused_computation.16 | convolution fusion | flops 3228565504 | bytes 12320768 | tf_op jit(solution)/shard_map/msncd,hncd->msh/dot_general | solution.py:77
  453.7 11.5 %bitcast_convert_fusion.1 = bf16[512,1024]{1,0:T(8,128)(2,1)} fusion(bf16[2,2048,1024]{2,1,0:T(8,128)(2,1)} %param.15, f32[2,2048,512]{2,1,0:T(8,128)} %copy-done.22), kind=kOutput, calls=%fused_computation.65 | convolution fusion | flops 4314365952 | bytes 17825792 | tf_op jit(solution)/shard_map/msf,msh->fh/dot_general | solution.py:62
  465.2 8.0 %bitcast_convert_fusion.3 = bf16[1024,2,3,64]{0,3,2,1:T(8,128)(2,1)} fusion(f32[1024]{0:T(1024)S(1)} %copy-done.15, f32[2,2048]{1,0:T(2,128)S(1)} %copy-done.11, f32[2,2048]{1,0:T(2,128)S(1)} %copy-done.13, bf16[2,2048,1024]{2,1,0:T(8,128)(2,1)} %param.13, bf16[2,2048,2,1,64]{1,4,2,0,3:T(8,128)(2,1)S(1)} %fusion.55, ...), kind=kOutput, calls=%fused_computation.67 | convolution fusion | flops 3245735936 | bytes 12357632 | tf_op jit(solution)/shard_map/msh,msncd->hncd/dot_general | solution.py:76
  473.2 16.4 %fusion.76 = bf16[2,64,1024]{2,1,0:T(8,128)(2,1)} fusion(bf16[2,2048,1024]{2,1,0:T(8,128)(2,1)} %copy-done.4, bf16[2,2,2048,2048]{2,3,1,0:T(8,128)(2,1)} %fusion.101, bf16[2,2048,2,3,64]{1,4,3,2,0:T(8,128)(2,1)} %fusion.39), kind=kOutput, calls=%fused_computation.69 | convolution fusion | flops 3221880832 | bytes 43253760 | tf_op jit(solution)/shard_map/msnd,msh->ndh/dot_general | solution.py:75
  489.6 139.6 %all-reduce.5.cloned.1.call-done = bf16[2,2048,1024]{2,1,0:T(8,128)(2,1)} async-done(((bf16[2,2048,1024]{2,1,0:T(8,128)(2,1)}), bf16[2,2048,1024]{2,1,0:T(8,128)(2,1)}) %all-reduce.5.cloned.1.call-update) | async-done | bytes 8388624 | tf_op jit(solution)/shard_map/psum | solution.py:78
  629.2 9.3 %fusion.17 = (f32[2,2048]{1,0:T(2,128)S(1)}, f32[2,2048]{1,0:T(2,128)S(1)}) fusion(bf16[2,2048,1024]{2,1,0:T(8,128)(2,1)} %all-reduce.5.cloned.1.call-done, f32[1024]{0:T(1024)S(1)} %copy-done.15, f32[2,2048]{1,0:T(2,128)S(1)} %copy-done.11, f32[2,2048]{1,0:T(2,128)S(1)} %copy-done.13, bf16[2,2048,1024]{2,1,0:T(8,128)(2,1)} %param.13), kind=kLoop, calls=%fused_computation.20 | loop fusion | flops 33546240 | bytes 16846848 | tf_op jit(solution)/shard_map/reduce_sum | solution.py:26
  638.5 12.5 %add_convert_fusion = bf16[2,2048,1024]{2,1,0:T(8,128)(2,1)} fusion(bf16[2,2048,1024]{2,1,0:T(8,128)(2,1)S(1)} %copy-done.6, bf16[2,2048,1024]{2,1,0:T(8,128)(2,1)} %param.13, bf16[2,2048,1024]{2,1,0:T(8,128)(2,1)} %copy-done.4, f32[2,2048]{1,0:T(2,128)S(1)} %broadcast_multiply_fusion, f32[2,2048]{1,0:T(2,128)S(1)} %broadcast_multiply_fusion.1, ...), kind=kLoop, calls=%fused_computation.17 | loop fusion | flops 50331648 | bytes 33624064 | tf_op jit(solution)/shard_map/convert_element_type | solution.py:80
  (63 shorter events, 3.7 us)
Async XLA Ops:
  7.2 205.4 %all-reduce.3.cloned.1.call-start = ((), (), s32[]{:S(2)}) async-start(), calls=%async_computation | async-start | bytes 16777216 | tf_op jit(solution)/shard_map/psum | solution.py:66
  8.4 8.3 %copy-start.7 = (bf16[2,2048,1024]{2,1,0:T(8,128)(2,1)S(1)}, bf16[2,2048,1024]{2,1,0:T(8,128)(2,1)}, u32[]{:S(2)}) copy-start(bf16[2,2048,1024]{2,1,0:T(8,128)(2,1)} %param.15) | copy-start | bytes 25165828
  8.4 8.3 %copy-start.17 = (bf16[512,1024]{1,0:T(8,128)(2,1)S(1)}, bf16[512,1024]{1,0:T(8,128)(2,1)}, u32[]{:S(2)}) copy-start(bf16[512,1024]{1,0:T(8,128)(2,1)} %param.25) | copy-start | bytes 3145732
  16.7 8.9 %copy-start.22 = (f32[2,2048,512]{2,1,0:T(8,128)}, f32[2,2048,512]{2,1,0:T(8,128)S(1)}, u32[]{:S(2)}) copy-start(f32[2,2048,512]{2,1,0:T(8,128)S(1)} %fusion.37) | copy-start | bytes 25165828
  34.4 594.8 %all-reduce.5.cloned.1.call-start = ((), (), s32[]{:S(2)}) async-start(), calls=%async_computation.1 | async-start | bytes 16777216 | tf_op jit(solution)/shard_map/psum | solution.py:78
  34.7 14.7 %slice-start = ((s8[8388608]{0:T(1024)(128)(4,1)}), s8[4194304]{0:T(1024)(128)(4,1)S(1)}, s32[]{:S(2)}) async-start(s8[8388608]{0:T(1024)(128)(4,1)} %bitcast.123), calls=%async_computation.2 | async-start | bytes 8388608
  38.9 10.6 %copy-start.16 = (bf16[1024]{0:T(1024)(128)(2,1)S(1)}, bf16[1024]{0:T(1024)(128)(2,1)}, u32[]{:S(2)}) copy-start(bf16[1024]{0:T(1024)(128)(2,1)} %param.20) | copy-start | bytes 6148
  38.9 10.6 %slice-start.1 = ((s8[8388608]{0:T(1024)(128)(4,1)}), s8[4194304]{0:T(1024)(128)(4,1)S(1)}, s32[]{:S(2)}) async-start(s8[8388608]{0:T(1024)(128)(4,1)} %bitcast.123), calls=%async_computation.3 | async-start | bytes 8388608
  38.9 10.6 %copy-start.10 = (f32[2,2048]{1,0:T(2,128)S(1)}, f32[2,2048]{1,0:T(2,128)}, u32[]{:S(2)}) copy-start(f32[2,2048]{1,0:T(2,128)} %param.17) | copy-start | bytes 49156
  38.9 10.6 %copy-start.12 = (f32[2,2048]{1,0:T(2,128)S(1)}, f32[2,2048]{1,0:T(2,128)}, u32[]{:S(2)}) copy-start(f32[2,2048]{1,0:T(2,128)} %param.16) | copy-start | bytes 49156
  38.9 10.6 %copy-start.18 = (bf16[1024,2,3,64]{0,3,2,1:T(8,128)(2,1)S(1)}, bf16[1024,2,3,64]{0,3,2,1:T(8,128)(2,1)}, u32[]{:S(2)}) copy-start(bf16[1024,2,3,64]{0,3,2,1:T(8,128)(2,1)} %param.22) | copy-start | bytes 2359300
  49.5 6.3 copy-start.14
  212.6 9.3 %copy-start.5 = (bf16[2,2048,1024]{2,1,0:T(8,128)(2,1)S(1)}, bf16[2,2048,1024]{2,1,0:T(8,128)(2,1)}, u32[]{:S(2)}) copy-start(bf16[2,2048,1024]{2,1,0:T(8,128)(2,1)} %all-reduce.3.cloned.1.call-done) | copy-start | bytes 25165828
  221.9 13.7 %copy-start.20 = (bf16[2,64,1024]{2,1,0:T(8,128)(2,1)S(1)}, bf16[2,64,1024]{2,1,0:T(8,128)(2,1)}, u32[]{:S(2)}) copy-start(bf16[2,64,1024]{2,1,0:T(8,128)(2,1)} %param.23) | copy-start | bytes 786436
  238.5 24.9 %copy-start.2 = (bf16[2,2048,2,64]{1,3,2,0:T(8,128)(2,1)}, bf16[2,2048,2,64]{1,3,2,0:T(8,128)(2,1)S(1)}, u32[]{:S(2)}) copy-start(bf16[2,2048,2,64]{1,3,2,0:T(8,128)(2,1)S(1)} %fusion.52) | copy-start | bytes 3145732
  346.6 83.4 %copy-start.3 = (bf16[2,2048,2,64]{1,3,2,0:T(8,128)(2,1)S(1)}, bf16[2,2048,2,64]{1,3,2,0:T(8,128)(2,1)}, u32[]{:S(2)}) copy-start(bf16[2,2048,2,64]{1,3,2,0:T(8,128)(2,1)} %copy-done.2) | copy-start | bytes 3145732
  429.9 15.0 %copy-start.19 = (bf16[1024,2,3,64]{0,3,2,1:T(8,128)(2,1)S(1)}, bf16[1024,2,3,64]{0,3,2,1:T(8,128)(2,1)}, u32[]{:S(2)}) copy-start(bf16[1024,2,3,64]{0,3,2,1:T(8,128)(2,1)} %param.22) | copy-start | bytes 2359300
  453.6 11.6 %copy-start.11 = (f32[2,2048]{1,0:T(2,128)S(1)}, f32[2,2048]{1,0:T(2,128)}, u32[]{:S(2)}) copy-start(f32[2,2048]{1,0:T(2,128)} %param.17) | copy-start | bytes 49156
  453.6 11.6 %copy-start.13 = (f32[2,2048]{1,0:T(2,128)S(1)}, f32[2,2048]{1,0:T(2,128)}, u32[]{:S(2)}) copy-start(f32[2,2048]{1,0:T(2,128)} %param.16) | copy-start | bytes 49156
  453.6 11.6 %copy-start.15 = (f32[1024]{0:T(1024)S(1)}, f32[1024]{0:T(1024)}, u32[]{:S(2)}) copy-start(f32[1024]{0:T(1024)} %copy-done.14) | copy-start | bytes 12292
  453.6 11.6 %copy-start.23 = (bf16[2,2048,2,1,64]{1,4,2,0,3:T(8,128)(2,1)S(1)}, bf16[2,2048,2,1,64]{1,4,2,0,3:T(8,128)(2,1)}, u32[]{:S(2)}) copy-start(bf16[2,2048,2,1,64]{1,4,2,0,3:T(8,128)(2,1)} %fusion.64) | copy-start | bytes 3145732
  453.6 11.6 %copy-start.24 = (bf16[2,2048,2,1,64]{1,4,2,0,3:T(8,128)(2,1)S(1)}, bf16[2,2048,2,1,64]{1,4,2,0,3:T(8,128)(2,1)}, u32[]{:S(2)}) copy-start(bf16[2,2048,2,1,64]{1,4,2,0,3:T(8,128)(2,1)} %fusion.61) | copy-start | bytes 3145732
  629.2 9.3 %copy-start.6 = (bf16[2,2048,1024]{2,1,0:T(8,128)(2,1)S(1)}, bf16[2,2048,1024]{2,1,0:T(8,128)(2,1)}, u32[]{:S(2)}) copy-start(bf16[2,2048,1024]{2,1,0:T(8,128)(2,1)} %all-reduce.5.cloned.1.call-done) | copy-start | bytes 25165828
  638.5 12.5 %copy-start.1 = (bf16[1024,512]{1,0:T(8,128)(2,1)S(1)}, bf16[1024,512]{1,0:T(8,128)(2,1)}, u32[]{:S(2)}) copy-start(bf16[1024,512]{1,0:T(8,128)(2,1)} %param.24) | copy-start | bytes 3145732
  (5 other events, 15.4 us)
Sparse Core Ops, SparseCore 0:
  34.5 178.0 all-reduce.2
  453.7 175.4 all-reduce.4
where the time goes:
time: 663 us; the launch traced here: 658 us
  matrix products  329 us (50%)
  waiting for transfers between devices  230 us (35%)
  other arithmetic  79.2 us (12%)
  between operations  14.6 us (2%)
    psum x1, waiting for transfers between devices, local_backward(): grad_norm_one = lax.psum(part_one, 'tp').astype(jnp.float32)  140 us
    psum x1, waiting for transfers between devices, local_backward(): grad_norm_two = lax.psum(part_two, 'tp').astype(jnp.float32)  89.9 us
    dot_general x1, matrix products, attention_backward(): wide_einsum('bnqk,bqnd->bknd', grad_s, q_heads).astype(jnp.bfloat16)  83.3 us
    dot_general x1, matrix products, attention_backward(): wide_einsum('bnqk,bknd->bqnd', grad_s, k_heads).astype(jnp.bfloat16)  83.2 us
    sub x1, matrix products, attention_backward(): attn_prob = jax.nn.softmax(jnp.where(causal, scores, -1e+30), axis=-1)  34.1 us
    convert_element_type x1, other arithmetic, attention_backward(): prob_bf16 = attn_prob.astype(jnp.bfloat16)  32.7 us
    dot_general x1, matrix products, attention_backward(): grad_p = wide_einsum('bqnd,bknd->bnqk', grad_o, v_heads)  24.8 us
    reduce_sum x2, other arithmetic, norm_backward(): mean_scaled = jnp.mean(scaled, axis=-1, keepdims=True)  18.5 us
  transfers between devices with their start and end apart: 2, of which 2 were waited for; matrix products, arithmetic and copies ran while one was open for 19% of the time, Pallas kernels for 0%

commit v1 on v0

v1 whole, which is shorter than its diff:
```python
import functools

import jax
import jax.numpy as jnp
from jax import lax
from jax.experimental import pallas as pl
from jax.experimental.pallas import tpu as pltpu
from jax.sharding import PartitionSpec as P

GELU_C = 0.7978845608028654
GELU_A = 0.044715
F32 = jnp.float32
BF16 = jnp.bfloat16
wide_einsum = functools.partial(jnp.einsum, preferred_element_type=F32)


def gelu_both(pre_act):
    sq = pre_act * pre_act
    tanh_val = jnp.tanh(GELU_C * pre_act * (1.0 + GELU_A * sq))
    half = 0.5 * (1.0 + tanh_val)
    value = pre_act * half
    slope = half + 0.5 * pre_act * (1.0 - tanh_val * tanh_val) * (GELU_C * (1.0 + 3.0 * GELU_A * sq))
    return value, slope


NT = (((1,), (1,)), ((), ()))
NN = (((1,), (0,)), ((), ()))


def dotf(a, b, dims=NN):
    return lax.dot_general(a, b, dims, preferred_element_type=F32)


def attention_kernel(blk, heads, dim, seq, qkv_ref, do_ref, o_ref, dqkv_ref, k_s, v_s, s_s, dp_s, dk_s, dv_s):
    scale = dim ** -0.5
    nb = seq // blk
    for n in range(heads):
        k_s[n] = qkv_ref[n, 1].astype(F32).T.astype(BF16)
        v_s[n] = qkv_ref[n, 2].astype(F32).T.astype(BF16)
        dk_s[n] = jnp.zeros_like(dk_s[n])
        dv_s[n] = jnp.zeros_like(dv_s[n])
    keep = (lax.broadcasted_iota(jnp.int32, (blk, blk), 0) <= lax.broadcasted_iota(jnp.int32, (blk, blk), 1))

    def fold(x, op):
        return op(x.reshape(blk // 8, 8, blk), axis=0)

    for i in range(nb):
        cols = pl.ds(i * blk, blk)
        q_t = [(qkv_ref[n, 0, :, cols].astype(F32) * scale).astype(BF16) for n in range(heads)]
        do_t = [do_ref[n, :, cols] for n in range(heads)]

        def pass_one(j, m, masked):
            rows = pl.ds(pl.multiple_of(j * blk, blk), blk)
            out = []
            for n in range(heads):
                s = dotf(k_s[n, rows], q_t[n])
                if masked:
                    s = jnp.where(keep, s, -1e30)
                s_s[n, rows] = s
                out.append(jnp.maximum(m[n], fold(s, jnp.max)))
            return tuple(out)

        m = tuple(jnp.full((8, blk), -jnp.inf, F32) for _ in range(heads))
        if i:
            m = lax.fori_loop(0, i, lambda j, c: pass_one(j, c, False), m)
        m = pass_one(i, m, True)
        m = [jnp.max(x, axis=0, keepdims=True) for x in m]

        def pass_two(j, carry):
            rows = pl.ds(pl.multiple_of(j * blk, blk), blk)
            out = []
            for n in range(heads):
                l, d = carry[n]
                dp = dotf(v_s[n, rows], do_t[n])
                e = jnp.exp(s_s[n, rows] - m[n])
                s_s[n, rows] = e
                dp_s[n, rows] = dp
                out.append((l + fold(e, jnp.sum), d + fold(e * dp, jnp.sum)))
            return tuple(out)

        zero = jnp.zeros((8, blk), F32)
        stats = lax.fori_loop(0, i + 1, pass_two, tuple((zero, zero) for _ in range(heads)))
        inv = [1.0 / jnp.sum(l, axis=0, keepdims=True) for l, _ in stats]
        dot_row = [jnp.sum(d, axis=0, keepdims=True) * inv[n] for n, (_, d) in enumerate(stats)]

        def pass_three(j, carry):
            rows = pl.ds(pl.multiple_of(j * blk, blk), blk)
            out = []
            for n in range(heads):
                o_t, dq_t = carry[n]
                p = s_s[n, rows] * inv[n]
                pb = p.astype(BF16)
                ds = (p * (dp_s[n, rows] - dot_row[n])).astype(BF16)
                dv_s[n, rows] += dotf(pb, do_t[n], NT)
                dk_s[n, rows] += dotf(ds, q_t[n], NT)
                o_t = o_t + dotf(qkv_ref[n, 2, :, rows], pb)
                dq_t = dq_t + dotf(qkv_ref[n, 1, :, rows], ds)
                out.append((o_t, dq_t))
            return tuple(out)

        zero = jnp.zeros((dim, blk), F32)
        acc = lax.fori_loop(0, i + 1, pass_three, tuple((zero, zero) for _ in range(heads)))
        for n in range(heads):
            o_ref[n, :, cols] = acc[n][0].astype(BF16)
            dqkv_ref[n, 0, :, cols] = (acc[n][1] * scale).astype(BF16)
    for n in range(heads):
        dqkv_ref[n, 1] = dk_s[n].T.astype(BF16)
        dqkv_ref[n, 2] = dv_s[n].T.astype(BF16)


def attention(qkv, grad_o):
    heads, _, dim, seq = qkv.shape
    blk = min(512, seq)
    vmem = pl.BlockSpec(memory_space=pltpu.VMEM)
    area = heads * seq * seq * dim
    return pl.pallas_call(
        functools.partial(attention_kernel, blk, heads, dim, seq),
        out_shape=(jax.ShapeDtypeStruct((heads, dim, seq), BF16), jax.ShapeDtypeStruct(qkv.shape, BF16)),
        in_specs=[vmem, vmem], out_specs=(vmem, vmem),
        scratch_shapes=[pltpu.VMEM((heads, seq, dim), BF16), pltpu.VMEM((heads, seq, dim), BF16),
                        pltpu.VMEM((heads, seq, blk), F32), pltpu.VMEM((heads, seq, blk), F32),
                        pltpu.VMEM((heads, seq, dim), F32), pltpu.VMEM((heads, seq, dim), F32)],
        compiler_params=pltpu.CompilerParams(vmem_limit_bytes=50 * 2 ** 20),
        cost_estimate=pl.CostEstimate(flops=24 * area, bytes_accessed=20 * heads * seq * dim, transcendentals=0),
        name="attention",
    )(qkv, grad_o)


MESH = pl.DeviceIdType.MESH
CHUNK = 128


def line_kernel(total, hidden, tasks_of, n_in, n_out, *refs):
    part, base_hbm, z_hbm, mu, rs, gain = refs[:6]
    task_in = refs[6:6 + n_in]
    out = refs[6 + n_in]
    task_out = refs[7 + n_in:7 + n_in + n_out]
    (pr, eb, acc, mb, base_v, z_v, mu_c, rs_c, lsem, p_snd, p_rcv, e_snd, e_rcv, m_snd, m_rcv, x_snd, x_rcv,
     y_snd, y_rcv, w_snd, w_rcv) = refs[7 + n_in + n_out:28 + n_in + n_out]
    task_scr = refs[28 + n_in + n_out:]
    half, quarter = total // 2, total // 4
    nk = quarter // CHUNK
    t = lax.axis_index('tp')
    c, z = lax.rem(t, 2), lax.div(t, 2)
    partner = t + 1 - 2 * c
    mate = 2 * (z + 1 - 2 * lax.rem(z, 2)) + c
    other = 2 * (3 - z) + c
    near = lax.div(z, 2)
    far = 1 - near
    is_mid = jnp.logical_or(z == 1, z == 2)
    is_end = jnp.logical_not(is_mid)

    def rows(s, k):
        return pl.ds(pl.multiple_of(s * quarter + k * CHUNK, CHUNK), CHUNK)

    def grows(cc, s, k):
        return pl.ds(pl.multiple_of(cc * half + s * quarter + k * CHUNK, CHUNK), CHUNK)

    def remote(src, dst, snd, rcv, dev):
        return pltpu.make_async_remote_copy(src_ref=src, dst_ref=dst, send_sem=snd, recv_sem=rcv,
                                            device_id={'tp': dev}, device_id_type=MESH)

    def p_copy(s, k):
        return remote(part.at[grows(1 - c, s, k)], pr.at[rows(s, k)], p_snd.at[s * nk + k], p_rcv.at[s * nk + k],
                      partner)

    def e_copy(s, k):
        return remote(acc.at[rows(s, k)], eb.at[rows(s, k)], e_snd.at[s * nk + k], e_rcv.at[s * nk + k], mate)

    def m_copy(k):
        return remote(acc.at[rows(far, k)], mb.at[pl.ds(k * CHUNK, CHUNK)], m_snd.at[k], m_rcv.at[k], other)

    def x_copy(s, k):
        here = out.at[grows(c, s, k)]
        return remote(here, here, x_snd.at[k], x_rcv.at[k], other)

    def y_copy(s, k):
        here = out.at[grows(c, s, k)]
        return remote(here, here, y_snd.at[s * nk + k], y_rcv.at[s * nk + k], mate)

    def w_copy(cc, s, k):
        here = out.at[grows(cc, s, k)]
        return remote(here, here, w_snd.at[s * nk + k], w_rcv.at[s * nk + k], partner)

    barrier = pltpu.get_barrier_semaphore()
    pl.semaphore_signal(barrier, inc=1, device_id={'tp': partner}, device_id_type=MESH)
    pl.semaphore_signal(barrier, inc=1, device_id={'tp': mate}, device_id_type=MESH)

    @pl.when(is_mid)
    def _():
        pl.semaphore_signal(barrier, inc=1, device_id={'tp': other}, device_id_type=MESH)
        own = pl.ds(pl.multiple_of(c * half + near * quarter, CHUNK), quarter)
        pltpu.make_async_copy(base_hbm.at[own], base_v, lsem.at[0]).start()
        pltpu.make_async_copy(z_hbm.at[own], z_v, lsem.at[1]).start()
        pl.semaphore_wait(barrier, 3)

    @pl.when(is_end)
    def _():
        pl.semaphore_wait(barrier, 2)

    for k in range(nk):
        for s in (far, near):
            p_copy(s, k).start()

    def summed(s, k, extra, i):
        r = pl.ds(pl.multiple_of(s * quarter + k * CHUNK + i * 16, 16), 16)
        g = pl.ds(pl.multiple_of(c * half + s * quarter + k * CHUNK + i * 16, 16), 16)
        tot = part[g, :].astype(F32) + pr[r, :].astype(F32)
        if extra:
            tot = tot + eb[r, :].astype(F32)
        return r, g, tot

    def add_rows(s, k, extra):
        @pl.loop(0, CHUNK // 16)
        def _(i):
            r, _g, tot = summed(s, k, extra, i)
            acc[r, :] = tot.astype(BF16)

    def far_event(k):
        p_copy(far, k).wait_recv()
        e_copy(far, k).wait_recv()
        add_rows(far, k, True)
        m_copy(k).start()

    def near_event(k):
        p_copy(near, k).wait_recv()
        e_copy(near, k).wait_recv()
        m_copy(k).wait_recv()
        if k == 0:
            pltpu.make_async_copy(base_hbm.at[pl.ds(0, quarter)], base_v, lsem.at[0]).wait()
            pltpu.make_async_copy(z_hbm.at[pl.ds(0, quarter)], z_v, lsem.at[1]).wait()
        stat = c * (half // CHUNK) + near * nk + k
        mu_c[...] = jnp.broadcast_to(mu[pl.ds(stat, 1), :], (CHUNK, CHUNK)).T
        rs_c[...] = jnp.broadcast_to(rs[pl.ds(stat, 1), :], (CHUNK, CHUNK)).T

        @pl.loop(0, CHUNK // 16)
        def _(i):
            _r, g, tot = summed(near, k, True, i)
            q = pl.ds(pl.multiple_of(k * CHUNK + i * 16, 16), 16)
            sub = pl.ds(pl.multiple_of(i * 16, 16), 16)
            u = (tot + mb[q, :].astype(F32)) * gain[...]
            r_col = rs_c[sub, :1]
            zhat = (z_v[q, :].astype(F32) - mu_c[sub, :1]) * r_col
            mean_u = jnp.sum(u, axis=1, keepdims=True) * (1.0 / hidden)
            mean_c = jnp.sum(u * zhat, axis=1, keepdims=True) * (1.0 / hidden)
            out[g, :] = (base_v[q, :].astype(F32) + r_col * (u - mean_u - zhat * mean_c)).astype(BF16)

        y_copy(near, k).start()
        x_copy(near, k).start()
        w_copy(c, near, k).start()

    def forward_event(k):
        x_copy(far, k).wait_recv()
        y_copy(far, k).start()
        w_copy(c, far, k).start()

    def end_send():
        for k in range(nk):
            for s in (far, near):
                p_copy(s, k).wait_recv()
                add_rows(s, k, False)
                e_copy(s, k).start()

    def end_relay(s, k):
        y_copy(s, k).wait_recv()
        w_copy(c, s, k).start()

    tasks = tasks_of(task_in, task_out, task_scr) if tasks_of else []
    steps = nk + 3
    share = -(-len(tasks) // steps) if tasks else 0
    for step in range(steps):
        @pl.when(is_mid)
        def _():
            if step < nk:
                far_event(step)
            if 0 <= step - 1 < nk:
                near_event(step - 1)
            if 0 <= step - 2 < nk:
                forward_event(step - 2)

        @pl.when(is_end)
        def _():
            if step == 0:
                end_send()
            if 0 <= step - 2 < nk:
                end_relay(near, step - 2)
            if 0 <= step - 3 < nk:
                end_relay(far, step - 3)

        for task in tasks[step * share:(step + 1) * share]:
            task()

    for k in range(nk):
        for s in (far, near):
            w_copy(1 - c, s, k).wait_recv()
            w_copy(c, s, k).wait_send()
            p_copy(s, k).wait_send()

    @pl.when(is_mid)
    def _():
        for k in range(nk):
            m_copy(k).wait_send()
            x_copy(near, k).wait_send()
            y_copy(near, k).wait_send()
            y_copy(far, k).wait_send()

    @pl.when(is_end)
    def _():
        for k in range(nk):
            for s in (far, near):
                e_copy(s, k).wait_send()


def line_reduce(part, base, z, mu, rs, gain, cid, tasks_of=None, task_in=(), task_out=(), task_scr=()):
    total, hidden = part.shape
    half, quarter = total // 2, total // 4
    n = half // CHUNK
    vmem = pl.BlockSpec(memory_space=pltpu.VMEM)
    hbm = pl.BlockSpec(memory_space=pl.ANY)
    sem = pltpu.SemaphoreType.DMA
    buf = pltpu.VMEM((half, hidden), BF16)
    buf_q = pltpu.VMEM((quarter, hidden), BF16)
    col = pltpu.VMEM((CHUNK, CHUNK), F32)
    outs = pl.pallas_call(
        functools.partial(line_kernel, total, hidden, tasks_of, len(task_in), len(task_out)),
        out_shape=(jax.ShapeDtypeStruct((total, hidden), BF16), *task_out),
        in_specs=[vmem, hbm, hbm, vmem, vmem, vmem] + [vmem] * len(task_in),
        out_specs=tuple([vmem] * (1 + len(task_out))),
        scratch_shapes=[buf, buf, buf, buf_q, buf_q, buf_q, col, col, sem((2,)),
                        sem((n,)), sem((n,)), sem((n,)), sem((n,)), sem((n // 2,)), sem((n // 2,)),
                        sem((n // 2,)), sem((n // 2,)), sem((n,)), sem((n,)), sem((n,)), sem((n,)), *task_scr],
        compiler_params=pltpu.CompilerParams(collective_id=cid, has_side_effects=True,
                                             vmem_limit_bytes=60 * 2 ** 20),
        name=f"line_reduce_{cid}",
    )(part, base, z, mu.reshape(total // CHUNK, CHUNK), rs.reshape(total // CHUNK, CHUNK),
      gain.astype(F32).reshape(1, hidden), *task_in)
    return outs


def solution(mesh):
    act_spec = P('dp', None, None)
    stat_spec = P('dp', None)
    in_specs = (act_spec, act_spec, act_spec, stat_spec, stat_spec, stat_spec, stat_spec, P(), P(),
                P(None, 'tp', None, None), P('tp', None, None), P(None, 'tp'), P('tp', None))
    out_specs = (act_spec, P('dp', 'tp', None, None), P(('dp', 'tp'), None, None), P('dp', 'tp'),
                 P(('dp', 'tp'), None))

    def local_backward(x_saved, h1_saved, grad_y, mean_one, rstd_one, mean_two, rstd_two,
                       gain_one, gain_two, w_qkv, w_out, w_up, w_down):
        mbs = x_saved.shape[0]
        zhat_two = (h1_saved.astype(F32) - mean_two[..., None]) * rstd_two[..., None]
        norm_two = (zhat_two * gain_two.astype(F32)).astype(BF16)
        act_out, grad_pre, part_two = [], [], []
        for b in range(mbs):
            value, slope = gelu_both(wide_einsum('sh,hf->sf', norm_two[b], w_up))
            act_out.append(value.astype(BF16))
            grad_pre.append((wide_einsum('sh,fh->sf', grad_y[b], w_down) * slope).astype(BF16))
            part_two.append(wide_einsum('sf,hf->sh', grad_pre[b], w_up).astype(BF16))
        grad_down = wide_einsum('msf,msh->fh', jnp.stack(act_out), grad_y).astype(BF16)
        grad_up = wide_einsum('msh,msf->hf', norm_two, jnp.stack(grad_pre)).astype(BF16)
        zhat_one = (x_saved.astype(F32) - mean_one[..., None]) * rstd_one[..., None]
        norm_one = (zhat_one * gain_one.astype(F32)).astype(BF16)
        grad_x, attn_out, grad_qkv, grad_h1 = [], [], [], []
        for b in range(mbs):
            dh, = line_reduce(part_two[b], grad_y[b], h1_saved[b], mean_two[b], rstd_two[b], gain_two, 2 * b)
            qkv = wide_einsum('sh,hncd->ncds', norm_one[b], w_qkv).astype(BF16)
            grad_o = wide_einsum('sh,ndh->nds', dh, w_out).astype(BF16)
            o, dqkv = attention(qkv, grad_o)
            part = wide_einsum('ncds,hncd->sh', dqkv, w_qkv).astype(BF16)
            dx, = line_reduce(part, dh, x_saved[b], mean_one[b], rstd_one[b], gain_one, 2 * b + 1)
            grad_x.append(dx)
            attn_out.append(o)
            grad_qkv.append(dqkv)
            grad_h1.append(dh)
        grad_out_w = wide_einsum('mnds,msh->ndh', jnp.stack(attn_out), jnp.stack(grad_h1)).astype(BF16)
        grad_qkv_w = wide_einsum('msh,mncds->hncd', norm_one, jnp.stack(grad_qkv)).astype(BF16)
        return jnp.stack(grad_x), grad_qkv_w, grad_out_w, grad_up, grad_down

    return jax.shard_map(local_backward, mesh=mesh, in_specs=in_specs, out_specs=out_specs, check_vma=False)
```

time: 663 us -> 483 us (0.73)
  Pallas kernels: 0 us -> 371 us
  matrix products: 329 us -> 60.2 us
  waiting for transfers between devices: 230 us -> 0 us
  other arithmetic: 79.2 us -> 23.9 us
  between operations: 14.6 us -> 1.36 us
  local copies, waits for them, and re-layouts: 5.7 us -> 18.7 us
    pallas_call x0 -> x6, Pallas kernels: none -> 371 us  [the longest x4 326 us: line_reduce(): pl.pallas_call(functools.partial(line_kernel, total, hidden, tasks_of, le...]
    dot_general x14, matrix products: 295 us -> 56.5 us  [the longest x2 9.06 us: local_backward(): wide_einsum('sh,fh->sf', grad_y[b], w_down) * slope]
    psum x2 -> x0, waiting for transfers between devices: 229 us -> none  [the longest x1 140 us: local_backward(): grad_norm_one = lax.psum(part_one, 'tp').astype(jnp.float32)]
    convert_element_type x5 -> x6, other arithmetic: 56.5 us -> 13.6 us  [the longest x2 6.16 us: local_backward(): norm_two = (zhat_two * gain_two.astype(F32)).astype(BF16)]
    sub x1 -> x0, matrix products: 34.1 us -> none  [attention_backward(): attn_prob = jax.nn.softmax(jnp.where(causal, scores, -1e+30), axis=-1)]
    reduce_sum x2 -> x0, other arithmetic: 18.5 us -> none  [norm_backward(): mean_scaled = jnp.mean(scaled, axis=-1, keepdims=True)]
    squeeze x0 -> x2, local copies, waits for them, and re-layouts: none -> 10.7 us  [the longest x1 6.09 us: local_backward(): h1_saved[b]]
    another operation x0 -> x2, other arithmetic: none -> 10.4 us  [the longest x1 7.7 us: local_backward(): return (jnp.stack(grad_x), grad_qkv_w, grad_out_w, grad_up, grad_down)]
  transfers between devices with their start and end apart: 2 -> 0, of which waited for: 2 -> 0; matrix products, arithmetic and copies ran while one was open for 19% -> 0% of each run, Pallas kernels for 0% -> 0%
where the time goes in v1:
time: 483 us; the launch traced here: 475 us
  Pallas kernels  371 us (77%)
  matrix products  60.2 us (12%)
  other arithmetic  23.9 us (5%)
  local copies, waits for them, and re-layouts  18.7 us (4%)
    pallas_call x4, Pallas kernels, line_reduce(): pl.pallas_call(functools.partial(line_kernel, total, hidden, tasks_of, le...  326 us
    pallas_call x2, Pallas kernels, attention(): pl.pallas_call(functools.partial(attention_kernel, blk, heads, dim, seq),...  45.2 us

profile of v1, /device:TPU:0, one launch (start us, length us, event | category | flops | bytes accessed | tf_op | source)
XLA Modules:
  0.0 475.0 jit_solution(10356327569277256148)
XLA Ops:
  7.7 5.5 %multiply_convert_fusion = bf16[2,2048,1024]{2,1,0:T(8,128)(2,1)S(1)} fusion(bf16[2,2048,1024]{2,1,0:T(8,128)(2,1)} %param.14, f32[1024]{0:T(1024)S(1)} %convert_element_type.84, f32[2,2048]{1,0:T(2,128)} %param.19, f32[2,2048]{1,0:T(2,128)} %param.18), kind=kLoop, calls=%fused_computation | loop fusion | flops 20971520 | bytes 16814080 | tf_op jit(solution)/shard_map/convert_element_type | solution.py:352
  13.3 2.4 fusion.3
  16.8 4.4 multiply_convert_fusion.4
  21.3 2.3 fusion.5
  23.6 2.7 fusion.34
  26.3 4.6 multiply_convert_fusion.5
  30.9 5.5 %bitcast_convert_fusion.3 = bf16[1024,512]{1,0:T(8,128)(2,1)} fusion(bf16[2,2048,1024]{2,1,0:T(8,128)(2,1)S(1)} %multiply_convert_fusion, bf16[1,2048,512]{2,1,0:T(8,128)(2,1)S(1)} %bitcast.157, bf16[1,2048,512]{2,1,0:T(8,128)(2,1)S(1)} %bitcast.158), kind=kOutput, calls=%fused_computation.53 | convolution fusion | flops 4297588736 | bytes 13631488 | tf_op jit(solution)/shard_map/msh,msf->hf/dot_general | solution.py:360
  36.4 5.6 %bitcast_convert_fusion.2 = bf16[512,1024]{1,0:T(8,128)(2,1)} fusion(bf16[2,2048,1024]{2,1,0:T(8,128)(2,1)S(1)} %copy-done.5, bf16[1,2048,512]{2,1,0:T(8,128)(2,1)S(1)} %get-tuple-element.30, bf16[1,2048,512]{2,1,0:T(8,128)(2,1)S(1)} %get-tuple-element.29), kind=kOutput, calls=%fused_computation.52 | convolution fusion | flops 4297588736 | bytes 13631488 | tf_op jit(solution)/shard_map/msf,msh->fh/dot_general | solution.py:359
  42.0 4.4 convolution_convert_fusion.1.refs_0_
  46.4 4.4 convolution_convert_fusion.refs_0_
  50.9 3.2 multiply_convert_fusion.1
  61.2 4.6 slice_bitcast_fusion.11
  66.9 6.1 %slice_bitcast_fusion.12 = (bf16[2048,1024]{1,0:T(8,128)(2,1)}, bf16[2048,1024]{1,0:T(8,128)(2,1)}, bf16[2048,1024]{1,0:T(8,128)(2,1)}, bf16[2048,1024]{1,0:T(8,128)(2,1)}) fusion(bf16[2,2048,1024]{2,1,0:T(8,128)(2,1)S(1)} %bitcast.136, bf16[2,2048,1024]{2,1,0:T(8,128)(2,1)S(1)} %copy-done.5), kind=kLoop, calls=%fused_computation.38 | loop fusion | bytes 33554432 | tf_op jit(solution)/shard_map/squeeze | solution.py:365
  73.0 83.7 %line_reduce_2.1.refs_1_ = bf16[2048,1024]{1,0:T(8,128)(2,1)} custom-call(bf16[2048,1024]{1,0:T(8,128)(2,1)} %convolution_convert_fusion.refs_0_, bf16[2048,1024]{1,0:T(8,128)(2,1)} %get-tuple-element.27.refs_1_, bf16[2048,1024]{1,0:T(8,128)(2,1)} %get-tuple-element.16.refs_2_, f32[16,128]{1,0:T(8,128)} %bitcast.153, f32[16,128]{1,0:T(8,128)} %bitcast.154, ...), custom_call_target="tpu_custom_call" | custom-call | tf_op jit(solution)/shard_map/line_reduce_2/pallas_call | solution.py:324
  156.7 80.7 %line_reduce_0.1.refs_1_ = bf16[2048,1024]{1,0:T(8,128)(2,1)} custom-call(bf16[2048,1024]{1,0:T(8,128)(2,1)} %convolution_convert_fusion.1.refs_0_, bf16[2048,1024]{1,0:T(8,128)(2,1)} %get-tuple-element.28.refs_1_, bf16[2048,1024]{1,0:T(8,128)(2,1)} %get-tuple-element.15.refs_2_, f32[16,128]{1,0:T(8,128)} %bitcast.151, f32[16,128]{1,0:T(8,128)} %bitcast.152, ...), custom_call_target="tpu_custom_call" | custom-call | tf_op jit(solution)/shard_map/line_reduce_0/pallas_call | solution.py:324
  237.4 3.7 fusion.31.do_ref
  241.1 22.6 %attention.2 = (bf16[2,64,2048]{2,1,0:T(8,128)(2,1)S(1)}, bf16[2,3,64,2048]{3,2,1,0:T(8,128)(2,1)S(1)}) custom-call(bf16[2,3,64,2048]{3,2,1,0:T(8,128)(2,1)} %convert_bitcast_fusion.1.qkv_ref, bf16[2,64,2048]{2,1,0:T(8,128)(2,1)S(1)} %fusion.31.do_ref), custom_call_target="tpu_custom_call" | custom-call | flops 12884901888 | bytes 5242880 | tf_op jit(solution)/shard_map/attention/pallas_call | solution.py:116
  265.2 22.6 %attention.3 = (bf16[2,64,2048]{2,1,0:T(8,128)(2,1)S(1)}, bf16[2,3,64,2048]{3,2,1,0:T(8,128)(2,1)S(1)}) custom-call(bf16[2,3,64,2048]{3,2,1,0:T(8,128)(2,1)} %convert_bitcast_fusion.qkv_ref, bf16[2,64,2048]{2,1,0:T(8,128)(2,1)S(1)} %fusion.28.do_ref), custom_call_target="tpu_custom_call" | custom-call | flops 12884901888 | bytes 5242880 | tf_op jit(solution)/shard_map/attention/pallas_call | solution.py:116
  289.9 6.8 %bitcast_convert_fusion.4 = bf16[1024,2,3,64]{0,3,2,1:T(8,128)(2,1)} fusion(bf16[1,2,3,64,2048]{4,3,2,1,0:T(8,128)(2,1)S(1)} %bitcast.130, bf16[1,2,3,64,2048]{4,3,2,1,0:T(8,128)(2,1)S(1)} %bitcast.129, bf16[2,2048,1024]{2,1,0:T(8,128)(2,1)} %copy-done.4), kind=kOutput, calls=%fused_computation.56 | convolution fusion | flops 3227910144 | bytes 12320768 | tf_op jit(solution)/shard_map/msh,mncds->hncd/dot_general | solution.py:376
  296.7 4.4 bitcast_convert_fusion.refs_0_
  301.1 80.7 %line_reduce_3.1 = bf16[2048,1024]{1,0:T(8,128)(2,1)} custom-call(bf16[2048,1024]{1,0:T(8,128)(2,1)} %bitcast_convert_fusion.refs_0_, bf16[2048,1024]{1,0:T(8,128)(2,1)} %line_reduce_2.1.refs_1_, bf16[2048,1024]{1,0:T(8,128)(2,1)} %get-tuple-element.14.refs_2_, f32[16,128]{1,0:T(8,128)} %bitcast.149, f32[16,128]{1,0:T(8,128)} %bitcast.150, f32[1,1024]{1,0:T(1,128)} %bitcast.143), custom_call_target="tpu_custom_call" | custom-call | tf_op jit(solution)/shard_map/line_reduce_3/pallas_call | solution.py:324
  381.8 4.4 bitcast_convert_fusion.1.refs_0_
  386.2 80.7 %line_reduce_1.1 = bf16[2048,1024]{1,0:T(8,128)(2,1)} custom-call(bf16[2048,1024]{1,0:T(8,128)(2,1)} %bitcast_convert_fusion.1.refs_0_, bf16[2048,1024]{1,0:T(8,128)(2,1)} %line_reduce_0.1.refs_1_, bf16[2048,1024]{1,0:T(8,128)(2,1)} %get-tuple-element.13.refs_2_, f32[16,128]{1,0:T(8,128)} %bitcast.147, f32[16,128]{1,0:T(8,128)} %bitcast.148, f32[1,1024]{1,0:T(1,128)} %bitcast.144), custom_call_target="tpu_custom_call" | custom-call | tf_op jit(solution)/shard_map/line_reduce_1/pallas_call | solution.py:324
  466.9 7.7 %pad_maximum_fusion = bf16[2,2048,1024]{2,1,0:T(8,128)(2,1)} fusion(bf16[1,2048,1024]{2,1,0:T(8,128)(2,1)} %bitcast.139, bf16[1,2048,1024]{2,1,0:T(8,128)(2,1)} %bitcast.140), kind=kLoop, calls=%fused_computation.4 | loop fusion | flops 4194304 | bytes 16777216 | tf_op jit(solution)/shard_map/stack | solution.py:377
  (48 shorter events, 20.2 us)
Async XLA Ops:
  0.6 12.6 %copy-start = (bf16[1024,512]{1,0:T(8,128)(2,1)S(1)}, bf16[1024,512]{1,0:T(8,128)(2,1)}, u32[]{:S(2)}) copy-start(bf16[1024,512]{1,0:T(8,128)(2,1)} %param.24) | copy-start | bytes 3145732
  1.4 49.4 %copy-start.8 = (f32[1024]{0:T(1024)}, f32[1024]{0:T(1024)S(1)}, u32[]{:S(2)}) copy-start(f32[1024]{0:T(1024)S(1)} %convert_element_type.79) | copy-start | bytes 12292
  2.1 11.1 %copy-start.9 = (f32[1024]{0:T(1024)}, f32[1024]{0:T(1024)S(1)}, u32[]{:S(2)}) copy-start(f32[1024]{0:T(1024)S(1)} %convert_element_type.84) | copy-start | bytes 12292
  13.2 3.4 copy-start.5
  13.2 3.6 copy-start.10
  42.0 8.8 %slice-start = ((s8[8388608]{0:T(1024)(128)(4,1)}), s8[4194304]{0:T(1024)(128)(4,1)S(1)}, s32[]{:S(2)}) async-start(s8[8388608]{0:T(1024)(128)(4,1)} %bitcast.133), calls=%async_computation | async-start | bytes 8388608
  46.4 4.4 slice-start.1
  46.4 4.4 copy-start.6
  46.4 4.4 copy-start.7
  50.8 3.2 copy-start.11
  54.1 3.9 copy-start.4
  59.8 5.9 %slice-start.2 = ((s8[8388608]{0:T(1024)(128)(4,1)}), s8[4194304]{0:T(1024)(128)(4,1)S(1)}, s32[]{:S(2)}) async-start(s8[8388608]{0:T(1024)(128)(4,1)} %bitcast.135), calls=%async_computation.2 | async-start | bytes 8388608
  61.2 5.7 %slice-start.3 = ((s8[8388608]{0:T(1024)(128)(4,1)}), s8[4194304]{0:T(1024)(128)(4,1)S(1)}, s32[]{:S(2)}) async-start(s8[8388608]{0:T(1024)(128)(4,1)} %bitcast.135), calls=%async_computation.3 | async-start | bytes 8388608
  156.7 80.7 %copy-start.12 = (bf16[2,64,1024]{2,1,0:T(8,128)(2,1)S(1)}, bf16[2,64,1024]{2,1,0:T(8,128)(2,1)}, u32[]{:S(2)}) copy-start(bf16[2,64,1024]{2,1,0:T(8,128)(2,1)} %param.23) | copy-start | bytes 786436
  241.1 22.6 %copy-start.3 = (bf16[2048,1024]{1,0:T(8,128)(2,1)S(1)}, bf16[2048,1024]{1,0:T(8,128)(2,1)}, u32[]{:S(2)}) copy-start(bf16[2048,1024]{1,0:T(8,128)(2,1)} %line_reduce_2.1.refs_1_) | copy-start | bytes 12582916
  265.2 22.7 %copy-start.2 = (bf16[2048,1024]{1,0:T(8,128)(2,1)S(1)}, bf16[2048,1024]{1,0:T(8,128)(2,1)}, u32[]{:S(2)}) copy-start(bf16[2048,1024]{1,0:T(8,128)(2,1)} %line_reduce_0.1.refs_1_) | copy-start | bytes 12582916
  466.9 7.7 %copy-start.1 = (bf16[1024,512]{1,0:T(8,128)(2,1)S(1)}, bf16[1024,512]{1,0:T(8,128)(2,1)}, u32[]{:S(2)}) copy-start(bf16[1024,512]{1,0:T(8,128)(2,1)} %param.24) | copy-start | bytes 3145732
